TPU v7x, 32 devices: a whole 2x2x4 slice. The times are simulated.
32 devices in a mesh: row: 4 (over x, core), col: 8 (over z, y).
Axes of the slice: x: 2, y: 2, z: 4, core: 2. Of those that a mesh axis runs over, the one named last changes fastest.
Arguments:
- momentum: float32 [5120, 27648], P('row', 'col'), may hold values from -130 to 130, as said below
- activations: bfloat16 [2048, 5120], P(None, 'row'), may hold values from -6 to 6
- out_grads: bfloat16 [2048, 27648], P(None, 'col'), may hold values from -0.125 to 0.125
- basis: float32 [27648, 256], P('col'), may hold values from -6 to 6
Outputs:
- new_momentum: float32 [5120, 27648], P('row', 'col')
- left_basis: float32 [5120, 256], P('row')
- new_basis: float32 [27648, 256], P('col')
Inputs may be any that keep to these rules, and one draw needn't show every extreme that they name: `momentum`: Real-valued entries of order one with varying row and column scales.
All inputs are finite; a program needn't handle non-finite values.
Results may differ from a plain program's by a relative error of at most 0.0003.
Values sent between devices are 32-bit elements; how exact they have to be, the bound alone decides.
No kernel may reach another device: no remote copies, remote signals or barrier semaphores. Data moves between devices by JAX's collectives and lax.ppermute only.
A program may use at most 128 MiB of HBM per device.

v0:
```python
import math
import jax
import jax.numpy as jnp
from jax import lax
from jax.sharding import PartitionSpec as P

D = 5120
F = 27648
EPS = 1e-06
HIGH = lax.Precision.HIGHEST


def left_product(block, factor_rows):
    return lax.dot_general(
        block,
        factor_rows,
        (((0,), (0,)), ((), ())),
        precision=HIGH,
        preferred_element_type=jnp.float32,
    )


def invert_gram(gram_total):
    factor = jnp.linalg.cholesky(gram_total)
    identity = jnp.eye(factor.shape[0], dtype=jnp.float32)
    return jax.scipy.linalg.solve_triangular(factor, identity, lower=True).T


def shards(momentum, activations, out_grads, basis):
    gradient = lax.dot_general(
        activations, out_grads, (((0,), (0,)), ((), ())), preferred_element_type=jnp.float32
    )
    merged = momentum + gradient
    block_rows = lax.psum(jnp.dot(merged, basis, precision=HIGH), "col")
    gram_part = jnp.dot(block_rows.T, block_rows, precision=HIGH)
    gram_total = lax.psum(gram_part, "row")
    inverse_t = invert_gram(gram_total)
    ortho = jnp.dot(block_rows, inverse_t, precision=HIGH)
    coeff_part = left_product(merged, ortho)
    coeffs = lax.psum(coeff_part, "row")
    squares = jnp.sum(coeffs * coeffs, axis=0)
    sq_total = lax.psum(squares, "col")
    new_momentum = merged - 0.5 * jnp.dot(ortho, coeffs.T, precision=HIGH)
    inv_norm = lax.rsqrt(sq_total / F + EPS)
    new_basis = coeffs * inv_norm[None, :]
    left_basis = ortho * jnp.float32(math.sqrt(D))
    return (new_momentum, left_basis, new_basis)


def solution(mesh):
    return jax.shard_map(
        shards,
        mesh=mesh,
        in_specs=(P("row", "col"), P(None, "row"), P(None, "col"), P("col", None)),
        out_specs=(P("row", "col"), P("row", None), P("col", None)),
        check_vma=False,
    )
```

profile of v0, /device:TPU:0, one launch (start us, length us, event | category | flops | bytes accessed | tf_op | source)
XLA Modules:
  0.0 406.0 jit_solution(12141631374180239289)
XLA Ops:
  7.2 29.5 %convolution_add_fusion = f32[1280,3456]{1,0:T(8,128)} fusion(f32[1280,3456]{1,0:T(8,128)} %param.4, bf16[2048,1280]{1,0:T(8,128)(2,1)} %param.5, bf16[2048,3456]{1,0:T(8,128)(2,1)} %param.6), kind=kOutput, calls=%fused_computation.2 | convolution fusion | flops 18123816960 | bytes 54788096 | tf_op jit(solution)/shard_map/dot_general | solution.py:30
  36.7 18.5 %fusion.15 = f32[1280,256]{1,0:T(8,128)} fusion(f32[1280,3456]{1,0:T(8,128)} %convolution_add_fusion, f32[3456,256]{1,0:T(8,128)S(1)} %copy-done), kind=kOutput, calls=%fused_computation.41 | convolution fusion | flops 13589544960 | bytes 22544384 | tf_op jit(solution)/shard_map/dot_general | solution.py:34
  55.2 0.2 all-reduce.7.cloned.1.call-start
  55.4 86.3 %all-reduce.5.cloned.1.call-done = f32[1280,256]{1,0:T(8,128)} async-done(((f32[1280,256]{1,0:T(8,128)}), f32[1280,256]{1,0:T(8,128)}) %all-reduce.5.cloned.1.call-update) | async-done | bytes 1310736 | tf_op jit(solution)/shard_map/psum | solution.py:34
  141.7 4.7 %fusion.16 = f32[256,256]{0,1:T(8,128)} fusion(f32[1280,256]{1,0:T(8,128)} %all-reduce.5.cloned.1.call-done), kind=kOutput, calls=%fused_computation.42 | convolution fusion | flops 1006632960 | bytes 1572864 | tf_op jit(solution)/shard_map/dot_general | solution.py:35
  146.5 0.0 all-reduce.9.cloned.1.call-start
  146.6 31.4 %all-reduce.7.cloned.1.call-done = f32[256,256]{0,1:T(8,128)} async-done(((f32[256,256]{0,1:T(8,128)}), f32[256,256]{0,1:T(8,128)}) %all-reduce.7.cloned.1.call-update) | async-done | bytes 262160 | tf_op jit(solution)/shard_map/psum | solution.py:36
  178.0 1.1 copy.8
  179.0 1.0 fusion.5
  180.0 11.7 %cholesky.50 = f32[128,128]{1,0:T(8,128)S(1)} custom-call(f32[128,128]{1,0:T(8,128)S(1)} %cholesky.118), custom_call_target="Cholesky" | custom-call | tf_op jit(solution)/shard_map/jit(cholesky)/cholesky | solution.py:24
  191.8 9.8 %custom-call.15 = f32[1,128,128]{1,2,0:T(8,128)S(1)} custom-call(f32[1,128,128]{2,1,0:T(8,128)S(1)} %get-tuple-element.24), custom_call_target="InvertDiagBlocksLowerTriangular" | custom-call | tf_op jit(solution)/shard_map/jit(cholesky)/cholesky | solution.py:24
  201.6 0.2 constant_dynamic-update-slice_fusion.1
  201.9 0.3 convolution_subtract_fusion.1
  202.1 11.7 %cholesky.105 = f32[128,128]{1,0:T(8,128)S(1)} custom-call(f32[128,128]{1,0:T(8,128)S(1)} %convolution_subtract_fusion.1), custom_call_target="Cholesky" | custom-call | tf_op jit(solution)/shard_map/jit(cholesky)/cholesky | solution.py:24
  213.9 0.7 compare_reduce_fusion
  215.9 0.1 triangular_solve.63
  215.9 4.2 %while.1 = (s32[]{:T(128)}, f32[256,256]{1,0:T(8,128)S(1)}, s32[2,2]{1,0:T(2,128)S(1)}, f32[2,128,128]{2,1,0:T(8,128)S(1)}, s32[]{:T(128)}) while((s32[]{:T(128)}, f32[256,256]{1,0:T(8,128)S(1)}, s32[2,2]{1,0:T(2,128)S(1)}, f32[2,128,128]{2,1,0:T(8,128)S(1)}, s32[]{:T(128)}) %tuple.28), condition=%wide.while_cond, body=%wide.while_body.sunk | while | flops 2 | bytes 131189 | solution.py:26
  216.2 0.6 fusion.34
  216.7 1.4 bitcast_dynamic-update-slice_fusion.2
  218.1 0.6 fusion.34
  218.7 1.4 bitcast_dynamic-update-slice_fusion.2
  220.1 19.7 %custom-call.16 = f32[2,128,128]{1,2,0:T(8,128)S(1)} custom-call(f32[2,128,128]{2,1,0:T(8,128)S(1)} %get-tuple-element.10), custom_call_target="InvertDiagBlocksLowerTriangular" | custom-call | tf_op jit(solution)/shard_map/jit(_solve_triangular)/triangular_solve | solution.py:26
  239.8 0.3 fusion.6
  240.1 0.3 convolution_subtract_fusion
  240.3 0.3 fusion.9
  240.7 2.3 broadcast_multiply_fusion.1
  242.9 32.2 %fusion.17 = f32[3456,256]{1,0:T(8,128)} fusion(f32[1280,3456]{1,0:T(8,128)} %convolution_add_fusion, f32[1280,256]{1,0:T(8,128)S(1)} %get-tuple-element.28), kind=kOutput, calls=%fused_computation.43 | convolution fusion | flops 13589544960 | bytes 22544384 | tf_op jit(solution)/shard_map/dot_general | solution.py:14
  275.2 75.0 %all-reduce.9.cloned.1.call-done = f32[3456,256]{1,0:T(8,128)} async-done(((f32[3456,256]{1,0:T(8,128)}), f32[3456,256]{1,0:T(8,128)}) %all-reduce.9.cloned.1.call-update) | async-done | bytes 3538960 | tf_op jit(solution)/shard_map/psum | solution.py:40
  350.1 2.5 multiply_reduce_fusion
  352.6 21.6 %psum.31 = f32[256]{0:T(256)S(1)} all-reduce(f32[256]{0:T(256)S(1)} %multiply_reduce_fusion), channel_id=1, replica_groups=mesh['row'=4,'col'=8] {'col'}, use_global_device_ids=true, to_apply=%region_8.9 | all-reduce | flops 256 | bytes 2048 | tf_op jit(solution)/shard_map/psum | solution.py:42
  374.2 22.7 %fusion = f32[1280,3456]{1,0:T(8,128)} fusion(f32[1280,3456]{1,0:T(8,128)} %convolution_add_fusion, f32[1280,256]{1,0:T(8,128)} %copy-done.3, f32[3456,256]{1,0:T(8,128)} %all-reduce.9.cloned.1.call-done), kind=kOutput, calls=%fused_computation.4 | convolution fusion | flops 13598392320 | bytes 40239104 | tf_op jit(solution)/shard_map/dot_general | solution.py:43
  397.0 2.0 broadcast_multiply_fusion
  (25 shorter events, 0.3 us)
Async XLA Ops:
  7.2 29.5 %copy-start = (f32[3456,256]{1,0:T(8,128)S(1)}, f32[3456,256]{1,0:T(8,128)}, u32[]{:S(2)}) copy-start(f32[3456,256]{1,0:T(8,128)} %param.7) | copy-start | bytes 10616836
  7.2 134.5 %all-reduce.5.cloned.1.call-start = ((), (), s32[]{:S(2)}) async-start(), calls=%async_computation | async-start | bytes 2621440 | tf_op jit(solution)/shard_map/psum | solution.py:34
  55.2 122.8 %all-reduce.7.cloned.1.call-start = ((), (), s32[]{:S(2)}) async-start(), calls=%async_computation.1 | async-start | bytes 524288 | tf_op jit(solution)/shard_map/psum | solution.py:36
  141.7 99.0 %copy-start.4 = (f32[1280,256]{1,0:T(8,128)S(1)}, f32[1280,256]{1,0:T(8,128)}, u32[]{:S(2)}) copy-start(f32[1280,256]{1,0:T(8,128)} %all-reduce.5.cloned.1.call-done) | copy-start | bytes 3932164
  146.5 203.7 %all-reduce.9.cloned.1.call-start = ((), (), s32[]{:S(2)}) async-start(), calls=%async_computation.2 | async-start | bytes 7077888 | tf_op jit(solution)/shard_map/psum | solution.py:40
  242.9 32.2 %copy-start.3 = (f32[1280,256]{1,0:T(8,128)}, f32[1280,256]{1,0:T(8,128)S(1)}, u32[]{:S(2)}) copy-start(f32[1280,256]{1,0:T(8,128)S(1)} %get-tuple-element.28) | copy-start | bytes 3932164
  374.2 22.7 %copy-start.2 = (f32[3456,256]{1,0:T(8,128)S(1)}, f32[3456,256]{1,0:T(8,128)}, u32[]{:S(2)}) copy-start(f32[3456,256]{1,0:T(8,128)} %all-reduce.9.cloned.1.call-done) | copy-start | bytes 10616836
  374.2 24.8 %copy-start.1 = (f32[3456,256]{1,0:T(8,128)S(1)}, f32[3456,256]{1,0:T(8,128)}, u32[]{:S(2)}) copy-start(f32[3456,256]{1,0:T(8,128)} %param.7) | copy-start | bytes 10616836
Sparse Core Ops, SparseCore 0:
  55.3 86.3 all-reduce.4
  146.6 31.3 all-reduce.6
  275.3 74.8 all-reduce.8
where the time goes:
time: 414 us; the launch traced here: 406 us
  waiting for transfers between devices  193 us (47%)
  matrix products  111 us (27%)
  other arithmetic  59.2 us (14%)
  blocking collectives  21.6 us (5%)
  between operations  15.6 us (4%)
  local copies, waits for them, and re-layouts  5.12 us (1%)
    psum x1, waiting for transfers between devices, shards(): block_rows = lax.psum(jnp.dot(merged, basis, precision=HIGH), 'col')  86.3 us
    psum x1, waiting for transfers between devices, shards(): coeffs = lax.psum(coeff_part, 'row')  75 us
    another operation x6, other arithmetic, invert_gram(): factor = jnp.linalg.cholesky(gram_total)  34 us
    dot_general x1, matrix products, left_product(): lax.dot_general(block, factor_rows, (((0,), (0,)), ((), ())), precision=H...  32.2 us
    psum x1, waiting for transfers between devices, shards(): gram_total = lax.psum(gram_part, 'row')  31.4 us
    dot_general x1, matrix products, shards(): lax.dot_general(activations, out_grads, (((0,), (0,)), ((), ())), preferr...  29.5 us
    dot_general x1, matrix products, shards(): new_momentum = merged - 0.5 * jnp.dot(ortho, coeffs.T, precision=HIGH)  22.7 us
    psum x1, blocking collectives, shards(): sq_total = lax.psum(squares, 'col')  21.6 us
  transfers between devices with their start and end apart: 3, of which 3 were waited for; matrix products, arithmetic and copies ran while one was open for 0% of the time, Pallas kernels for 0%

commit v1 on v0

--- a/solution.py
+++ b/solution.py
@@ -37,7 +37,11 @@
     inverse_t = invert_gram(gram_total)
     ortho = jnp.dot(block_rows, inverse_t, precision=HIGH)
     coeff_part = left_product(merged, ortho)
-    coeffs = lax.psum(coeff_part, "row")
+    size = lax.axis_size("row")
+    coeffs, far = (coeff_part, 1)
+    while far < size:
+        coeffs = coeffs + lax.ppermute(coeffs, "row", [(i, i ^ far) for i in range(size)])
+        far = 2 * far
     squares = jnp.sum(coeffs * coeffs, axis=0)
     sq_total = lax.psum(squares, "col")
     new_momentum = merged - 0.5 * jnp.dot(ortho, coeffs.T, precision=HIGH)

time: 414 us -> 421 us (1.017)
  waiting for transfers between devices: 193 us -> 202 us
    ppermute x0 -> x2, waiting for transfers between devices: none -> 84.7 us  [shards(): lax.ppermute(coeffs, 'row', [(i, i ^ far) for i in range(size)])]
    psum x1 -> x0, waiting for transfers between devices: 75 us -> none  [shards(): coeffs = lax.psum(coeff_part, 'row')]
  transfers between devices with their start and end apart: 3 -> 4, of which waited for: 3 -> 4; matrix products, arithmetic and copies ran while one was open for 0% -> 0% of each run, Pallas kernels for 0% -> 0%
where the time goes in v1:
time: 421 us; the launch traced here: 413 us
  waiting for transfers between devices  202 us (48%)
  matrix products  107 us (25%)
  other arithmetic  60.4 us (14%)
  blocking collectives  21.3 us (5%)
  between operations  16 us (4%)
  local copies, waits for them, and re-layouts  5.23 us (1%)
    psum x1, waiting for transfers between devices, shards(): block_rows = lax.psum(jnp.dot(merged, basis, precision=HIGH), 'col')  86.3 us
    ppermute x2, waiting for transfers between devices, shards(): lax.ppermute(coeffs, 'row', [(i, i ^ far) for i in range(size)])  84.7 us
    another operation x6, other arithmetic, invert_gram(): factor = jnp.linalg.cholesky(gram_total)  34.2 us
    psum x1, waiting for transfers between devices, shards(): gram_total = lax.psum(gram_part, 'row')  31.4 us
    dot_general x1, matrix products, left_product(): lax.dot_general(block, factor_rows, (((0,), (0,)), ((), ())), precision=H...  30.9 us
    dot_general x1, matrix products, shards(): lax.dot_general(activations, out_grads, (((0,), (0,)), ((), ())), preferr...  29.5 us
    psum x1, blocking collectives, shards(): sq_total = lax.psum(squares, 'col')  21.3 us
    another operation x3, other arithmetic, invert_gram(): return jax.scipy.linalg.solve_triangular(factor, identity, lower=True).T  19.7 us
  transfers between devices with their start and end apart: 4, of which 4 were waited for; matrix products, arithmetic and copies ran while one was open for 0% of the time, Pallas kernels for 0%

profile of v1, /device:TPU:0, one launch (start us, length us, event | category | flops | bytes accessed | tf_op | source)
XLA Modules:
  0.0 412.8 jit_solution(16189179372167860639)
XLA Ops:
  7.2 29.5 %convolution_add_fusion = f32[1280,3456]{1,0:T(8,128)} fusion(f32[1280,3456]{1,0:T(8,128)} %param.4, bf16[2048,1280]{1,0:T(8,128)(2,1)} %param.5, bf16[2048,3456]{1,0:T(8,128)(2,1)} %param.6), kind=kOutput, calls=%fused_computation.2 | convolution fusion | flops 18123816960 | bytes 54788096 | tf_op jit(solution)/shard_map/dot_general | solution.py:30
  36.7 18.5 %fusion.15 = f32[1280,256]{1,0:T(8,128)} fusion(f32[1280,3456]{1,0:T(8,128)} %convolution_add_fusion, f32[3456,256]{1,0:T(8,128)S(1)} %copy-done), kind=kOutput, calls=%fused_computation.41 | convolution fusion | flops 13589544960 | bytes 22544384 | tf_op jit(solution)/shard_map/dot_general | solution.py:34
  55.2 0.2 all-reduce.6.cloned.1.call-start
  55.4 86.3 %all-reduce.4.cloned.1.call-done = f32[1280,256]{1,0:T(8,128)} async-done(((f32[1280,256]{1,0:T(8,128)}), f32[1280,256]{1,0:T(8,128)}) %all-reduce.4.cloned.1.call-update) | async-done | bytes 1310736 | tf_op jit(solution)/shard_map/psum | solution.py:34
  141.7 4.8 %fusion.16 = f32[256,256]{0,1:T(8,128)} fusion(f32[1280,256]{1,0:T(8,128)} %all-reduce.4.cloned.1.call-done), kind=kOutput, calls=%fused_computation.42 | convolution fusion | flops 1006632960 | bytes 1572864 | tf_op jit(solution)/shard_map/dot_general | solution.py:35
  146.6 31.4 %all-reduce.6.cloned.1.call-done = f32[256,256]{0,1:T(8,128)} async-done(((f32[256,256]{0,1:T(8,128)}), f32[256,256]{0,1:T(8,128)}) %all-reduce.6.cloned.1.call-update) | async-done | bytes 262160 | tf_op jit(solution)/shard_map/psum | solution.py:36
  178.0 1.1 copy.8
  179.1 1.0 fusion.5
  180.1 11.7 %cholesky.50 = f32[128,128]{1,0:T(8,128)S(1)} custom-call(f32[128,128]{1,0:T(8,128)S(1)} %cholesky.118), custom_call_target="Cholesky" | custom-call | tf_op jit(solution)/shard_map/jit(cholesky)/cholesky | solution.py:24
  191.8 9.8 %custom-call.15 = f32[1,128,128]{1,2,0:T(8,128)S(1)} custom-call(f32[1,128,128]{2,1,0:T(8,128)S(1)} %get-tuple-element.26), custom_call_target="InvertDiagBlocksLowerTriangular" | custom-call | tf_op jit(solution)/shard_map/jit(cholesky)/cholesky | solution.py:24
  201.7 0.2 constant_dynamic-update-slice_fusion.1
  201.9 0.3 convolution_subtract_fusion.1
  202.2 11.9 %cholesky.105 = f32[128,128]{1,0:T(8,128)S(1)} custom-call(f32[128,128]{1,0:T(8,128)S(1)} %convolution_subtract_fusion.1), custom_call_target="Cholesky" | custom-call | tf_op jit(solution)/shard_map/jit(cholesky)/cholesky | solution.py:24
  214.1 0.7 compare_reduce_fusion
  216.2 4.0 while.1
  216.2 0.6 fusion.34
  216.8 1.4 bitcast_dynamic-update-slice_fusion.2
  218.3 0.6 fusion.34
  218.9 1.4 bitcast_dynamic-update-slice_fusion.2
  220.3 19.7 %custom-call.16 = f32[2,128,128]{1,2,0:T(8,128)S(1)} custom-call(f32[2,128,128]{2,1,0:T(8,128)S(1)} %get-tuple-element.10), custom_call_target="InvertDiagBlocksLowerTriangular" | custom-call | tf_op jit(solution)/shard_map/jit(_solve_triangular)/triangular_solve | solution.py:26
  240.0 0.3 fusion.6
  240.2 0.3 convolution_subtract_fusion
  240.5 0.3 fusion.9
  240.8 2.3 broadcast_multiply_fusion.1
  243.1 30.9 %fusion.17 = f32[3456,256]{1,0:T(8,128)S(1)} fusion(f32[1280,3456]{1,0:T(8,128)} %convolution_add_fusion, f32[1280,256]{1,0:T(8,128)S(1)} %get-tuple-element.30), kind=kOutput, calls=%fused_computation.43 | convolution fusion | flops 13589544960 | bytes 22544384 | tf_op jit(solution)/shard_map/dot_general | solution.py:14
  274.2 6.2 %collective-permute-done = f32[3456,256]{1,0:T(8,128)S(1)} collective-permute-done((f32[3456,256]{1,0:T(8,128)S(1)}, f32[3456,256]{1,0:T(8,128)S(1)}, u32[]{:S(2)}, u32[]{:S(2)}) %collective-permute-start) | collective-permute-done | bytes 3538976 | tf_op jit(solution)/shard_map/ppermute | solution.py:43
  280.4 0.5 add.46
  280.9 78.5 %collective-permute-done.1 = f32[3456,256]{1,0:T(8,128)S(1)} collective-permute-done((f32[3456,256]{1,0:T(8,128)S(1)}, f32[3456,256]{1,0:T(8,128)S(1)}, u32[]{:S(2)}, u32[]{:S(2)}) %collective-permute-start.1) | collective-permute-done | bytes 3538976 | tf_op jit(solution)/shard_map/ppermute | solution.py:43
  359.5 0.8 multiply_reduce_fusion
  360.4 19.6 %fusion = f32[1280,3456]{1,0:T(8,128)} fusion(f32[1280,3456]{1,0:T(8,128)S(1)} %bitcast.43, f32[1280,256]{1,0:T(8,128)S(1)} %get-tuple-element.30, f32[3456,256]{1,0:T(8,128)S(1)} %get-tuple-element.20), kind=kOutput, calls=%fused_computation.4 | convolution fusion | flops 13598392320 | bytes 40239104 | tf_op jit(solution)/shard_map/dot_general | solution.py:47
  380.0 21.3 %psum.23 = f32[256]{0:T(256)S(1)} all-reduce(f32[256]{0:T(256)S(1)} %get-tuple-element.19), channel_id=1, replica_groups=mesh['row'=4,'col'=8] {'col'}, use_global_device_ids=true, to_apply=%region_7.8 | all-reduce | flops 256 | bytes 2048 | tf_op jit(solution)/shard_map/psum | solution.py:46
  401.3 4.2 %broadcast_multiply_fusion = f32[3456,256]{1,0:T(8,128)} fusion(f32[3456,256]{1,0:T(8,128)} %copy-done.2, f32[256]{0:T(256)S(1)} %add_rsqrt_fusion), kind=kLoop, calls=%fused_computation.6 | loop fusion | flops 884736 | bytes 7078912 | tf_op jit(solution)/shard_map/mul | solution.py:49
  (36 shorter events, 0.5 us)
Async XLA Ops:
  7.2 29.5 %copy-start = (f32[3456,256]{1,0:T(8,128)S(1)}, f32[3456,256]{1,0:T(8,128)}, u32[]{:S(2)}) copy-start(f32[3456,256]{1,0:T(8,128)} %param.7) | copy-start | bytes 10616836
  7.2 134.5 %all-reduce.4.cloned.1.call-start = ((), (), s32[]{:S(2)}) async-start(), calls=%async_computation | async-start | bytes 2621440 | tf_op jit(solution)/shard_map/psum | solution.py:34
  55.2 122.8 %all-reduce.6.cloned.1.call-start = ((), (), s32[]{:S(2)}) async-start(), calls=%async_computation.1 | async-start | bytes 524288 | tf_op jit(solution)/shard_map/psum | solution.py:36
  141.7 99.1 %copy-start.3 = (f32[1280,256]{1,0:T(8,128)S(1)}, f32[1280,256]{1,0:T(8,128)}, u32[]{:S(2)}) copy-start(f32[1280,256]{1,0:T(8,128)} %all-reduce.4.cloned.1.call-done) | copy-start | bytes 3932164
  243.1 117.2 %slice-start = ((s8[17694720]{0:T(1024)(128)(4,1)}), s8[4194304]{0:T(1024)(128)(4,1)S(1)}, s32[]{:S(2)}) async-start(s8[17694720]{0:T(1024)(128)(4,1)} %bitcast.42), calls=%async_computation.2 | async-start | bytes 8388608
  243.1 117.2 %slice-start.1 = ((s8[17694720]{0:T(1024)(128)(4,1)}), s8[4194304]{0:T(1024)(128)(4,1)S(1)}, s32[]{:S(2)}) async-start(s8[17694720]{0:T(1024)(128)(4,1)} %bitcast.42), calls=%async_computation.3 | async-start | bytes 8388608
  243.1 117.2 %slice-start.2 = ((s8[17694720]{0:T(1024)(128)(4,1)}), s8[4194304]{0:T(1024)(128)(4,1)S(1)}, s32[]{:S(2)}) async-start(s8[17694720]{0:T(1024)(128)(4,1)} %bitcast.42), calls=%async_computation.4 | async-start | bytes 8388608
  274.1 86.3 %slice-start.3 = ((s8[17694720]{0:T(1024)(128)(4,1)}), s8[4194304]{0:T(1024)(128)(4,1)S(1)}, s32[]{:S(2)}) async-start(s8[17694720]{0:T(1024)(128)(4,1)} %bitcast.42), calls=%async_computation.5 | async-start | bytes 8388608
  274.1 6.3 %collective-permute-start = (f32[3456,256]{1,0:T(8,128)S(1)}, f32[3456,256]{1,0:T(8,128)S(1)}, u32[]{:S(2)}, u32[]{:S(2)}) collective-permute-start(f32[3456,256]{1,0:T(8,128)S(1)} %fusion.17), channel_id=1, source_target_pairs={{0,8},{8,0},{16,24},{24,16},{1,9},{9,1},{17,25},{25,17},{2,10},{10... | collective-permute-start | bytes 10616840 | tf_op jit(solution)/shard_map/ppermute | solution.py:43
  280.8 79.5 %slice-start.4 = ((s8[17694720]{0:T(1024)(128)(4,1)}), s8[917504]{0:T(1024)(128)(4,1)S(1)}, s32[]{:S(2)}) async-start(s8[17694720]{0:T(1024)(128)(4,1)} %bitcast.42), calls=%async_computation.6 | async-start | bytes 1835008
  280.8 78.6 %collective-permute-start.1 = (f32[3456,256]{1,0:T(8,128)S(1)}, f32[3456,256]{1,0:T(8,128)S(1)}, u32[]{:S(2)}, u32[]{:S(2)}) collective-permute-start(f32[3456,256]{1,0:T(8,128)S(1)} %add.46), channel_id=1, source_target_pairs={{0,16},{8,24},{16,0},{24,8},{1,17},{9,25},{17,1},{25,9},{2,18},{10... | collective-permute-start | bytes 10616840 | tf_op jit(solution)/shard_map/ppermute | solution.py:43
  360.3 19.7 %copy-start.2 = (f32[3456,256]{1,0:T(8,128)}, f32[3456,256]{1,0:T(8,128)S(1)}, u32[]{:S(2)}) copy-start(f32[3456,256]{1,0:T(8,128)S(1)} %get-tuple-element.20) | copy-start | bytes 10616836
  401.3 4.2 %copy-start.1 = (f32[3456,256]{1,0:T(8,128)S(1)}, f32[3456,256]{1,0:T(8,128)}, u32[]{:S(2)}) copy-start(f32[3456,256]{1,0:T(8,128)} %param.7) | copy-start | bytes 10616836
Sparse Core Ops, SparseCore 0:
  55.3 86.3 all-reduce.3
  146.6 31.3 all-reduce.5
